TPU v7x, 32 devices: a whole 2x2x4 slice. The times are simulated.
32 devices in a mesh: fsdp: 8 (over z, x), grp: 4 (over y, core).
Axes of the slice: x: 2, y: 2, z: 4, core: 2. Of those that a mesh axis runs over, the one named last changes fastest.
Arguments:
- grad: bfloat16 [28672, 8192], P('fsdp', 'grp'), may hold values from -6 to 6
- projector_t: bfloat16 [1024, 8192], P('fsdp', 'grp'), may hold values from -0.0625 to 0.0625
- first_moment: float32 [28672, 1024], P('fsdp', 'grp'), may hold values from -3 to 3
- second_moment: float32 [28672, 1024], P('fsdp', 'grp'), may hold values from 0.0001 to 0.01
Outputs:
- update: float32 [28672, 8192], P('fsdp', 'grp')
- first_new: float32 [28672, 1024], P('fsdp', 'grp')
- second_new: float32 [28672, 1024], P('fsdp', 'grp')
All inputs are finite; a program needn't handle non-finite values.
Results may differ from a plain program's by a relative error of at most 0.0029.
Values may be sent and summed in bfloat16 or wider, within the bound.
A program may use at most 128 MiB of HBM per device.

v0:
```python
import jax
import jax.numpy as jnp
from jax import lax
from jax.sharding import PartitionSpec as P

STEP = 10


def body(grad, projector_t, first_moment, second_moment):
    whole = lax.all_gather(projector_t, "fsdp", axis=0, tiled=True)
    partial_value = lax.dot_general(
        grad, whole, (((1,), (1,)), ((), ())), preferred_element_type=jnp.float32
    )
    projected = lax.psum_scatter(partial_value, "grp", scatter_dimension=1, tiled=True)
    first_new = 0.9 * first_moment + 0.1 * projected
    second_new = 0.999 * second_moment + 0.001 * projected * projected
    correct_one = 1.0 - 0.9**STEP
    correct_two = 1.0 - 0.999**STEP
    normalized = (first_new / correct_one / (jnp.sqrt(second_new / correct_two) + 1e-08)).astype(
        jnp.bfloat16
    )
    full_step = lax.all_gather(normalized, "grp", axis=1, tiled=True)
    update = jnp.dot(full_step, whole, preferred_element_type=jnp.float32)
    return (update, first_new, second_new)


def solution(mesh):
    return jax.shard_map(
        body,
        mesh=mesh,
        in_specs=(P("fsdp", "grp"), P("fsdp", "grp"), P("fsdp", "grp"), P("fsdp", "grp")),
        out_specs=(P("fsdp", "grp"), P("fsdp", "grp"), P("fsdp", "grp")),
        check_vma=False,
    )
```

profile of v0, /device:TPU:0, one launch (start us, length us, event | category | flops | bytes accessed | tf_op | source)
XLA Modules:
  0.0 306.6 jit_solution(5147989194662069620)
XLA Ops:
  7.2 0.0 all-gather.3.cloned.1.call-start
  7.2 0.7 all-gather.3.cloned.1.call-update
  7.9 0.0 reduce-scatter.2.cloned.1.call-start
  7.9 77.7 %all-gather.3.cloned.1.call-done = bf16[1024,2048]{1,0:T(8,128)(2,1)} async-done(((bf16[128,2048]{1,0:T(8,128)(2,1)}), bf16[1024,2048]{1,0:T(8,128)(2,1)}) %all-gather.3.cloned.1.call-update) | async-done | bytes 4194320 | tf_op jit(solution)/shard_map/all_gather | solution.py:10
  85.6 21.8 %fusion.2 = f32[3584,1024]{1,0:T(8,128)} fusion(bf16[3584,2048]{1,0:T(8,128)(2,1)} %param.4, bf16[1024,2048]{1,0:T(8,128)(2,1)} %all-gather.3.cloned.1.call-done), kind=kOutput, calls=%fused_computation.4 | convolution fusion | flops 15032385536 | bytes 33554432 | tf_op jit(solution)/shard_map/dot_general | solution.py:11
  107.5 0.0 reduce-scatter.2.cloned.1.call-update
  107.5 0.0 all-gather.5.cloned.1.call-start
  107.6 108.7 %reduce-scatter.2.cloned.1.call-done = f32[3584,256]{1,0:T(8,128)} async-done(((f32[3584,1024]{1,0:T(8,128)}), f32[3584,256]{1,0:T(8,128)}) %reduce-scatter.2.cloned.1.call-update) | async-done | bytes 3670032 | tf_op jit(solution)/shard_map/reduce_scatter | solution.py:14
  216.3 7.7 %divide_convert_fusion = (bf16[3584,256]{1,0:T(8,128)(2,1)}, f32[3584,256]{1,0:T(8,128)}, f32[3584,256]{1,0:T(8,128)}) fusion(f32[3584,256]{1,0:T(8,128)} %reduce-scatter.2.cloned.1.call-done, f32[3584,256]{1,0:T(8,128)} %param.6, f32[3584,256]{1,0:T(8,128)} %param.7), kind=kLoop, calls=%fused_computation.2 | loop fusion | flops 11010048 | bytes 20185088 | tf_op jit(solution)/shard_map/convert_element_type | solution.py:19
  224.0 0.0 all-gather.5.cloned.1.call-update
  224.0 53.4 %all-gather.5.cloned.1.call-done = bf16[3584,1024]{1,0:T(8,128)(2,1)} async-done(((bf16[3584,256]{1,0:T(8,128)(2,1)}), bf16[3584,1024]{1,0:T(8,128)(2,1)}) %all-gather.5.cloned.1.call-update) | async-done | bytes 7340048 | tf_op jit(solution)/shard_map/all_gather | solution.py:22
  277.5 22.6 %fusion.3 = f32[3584,2048]{1,0:T(8,128)} fusion(bf16[3584,1024]{1,0:T(8,128)(2,1)} %all-gather.5.cloned.1.call-done, bf16[1024,2048]{1,0:T(8,128)(2,1)} %all-gather.3.cloned.1.call-done), kind=kOutput, calls=%fused_computation.5 | convolution fusion | flops 15032385536 | bytes 40894464 | tf_op jit(solution)/shard_map/dot_general | solution.py:23
Async XLA Ops:
  7.2 78.5 %all-gather.3.cloned.1.call-start = ((), (), s32[]{:S(2)}) async-start(), calls=%async_computation.1 | async-start | bytes 4718592 | tf_op jit(solution)/shard_map/all_gather | solution.py:10
  7.9 208.4 %reduce-scatter.2.cloned.1.call-start = ((), (), s32[]{:S(2)}) async-start(), calls=%async_computation.2 | async-start | bytes 18350080 | tf_op jit(solution)/shard_map/reduce_scatter | solution.py:14
  107.5 170.0 %all-gather.5.cloned.1.call-start = ((), (), s32[]{:S(2)}) async-start(), calls=%async_computation.3 | async-start | bytes 9175040 | tf_op jit(solution)/shard_map/all_gather | solution.py:22
Sparse Core Ops, SparseCore 0:
  10.1 75.4 all-gather.2
  107.6 108.6 reduce-scatter.1
  224.2 53.2 all-gather.4
where the time goes:
time: 307 us
  waiting for transfers between devices  241 us (79%)
  matrix products  44.4 us (14%)
  between operations  13.7 us (4%)
  other arithmetic  7.72 us (3%)
    reduce_scatter x1, waiting for transfers between devices, body(): lax.psum_scatter(partial_value, 'grp', scatter_dimension=1, tiled=True)  109 us
    all_gather x1, waiting for transfers between devices, body(): whole = lax.all_gather(projector_t, 'fsdp', axis=0, tiled=True)  77.7 us
    all_gather x1, waiting for transfers between devices, body(): full_step = lax.all_gather(normalized, 'grp', axis=1, tiled=True)  53.4 us
    dot_general x1, matrix products, body(): update = jnp.dot(full_step, whole, preferred_element_type=jnp.float32)  22.6 us
    dot_general x1, matrix products, body(): lax.dot_general(grad, whole, (((1,), (1,)), ((), ())), preferred_element_...  21.8 us
    convert_element_type x1, other arithmetic, body(): (first_new / correct_one / (jnp.sqrt(second_new / correct_two) + 1e-08))....  7.72 us
  transfers between devices with their start and end apart: 3, of which 3 were waited for; matrix products, arithmetic and copies ran while one was open for 0% of the time, Pallas kernels for 0%

commit v1 on v0

--- a/solution.py
+++ b/solution.py
@@ -1,9 +1,17 @@
+import functools
 import jax
 import jax.numpy as jnp
 from jax import lax
 from jax.sharding import PartitionSpec as P
 
 STEP = 10
+
+
+def form_screen(w_in, across):
+    return jnp.concatenate(lax.all_gather(w_in, across), axis=1)
+
+
+face_hold = functools.partial(form_screen, across="grp")
 
 
 def body(grad, projector_t, first_moment, second_moment):
@@ -19,7 +27,7 @@
     normalized = (first_new / correct_one / (jnp.sqrt(second_new / correct_two) + 1e-08)).astype(
         jnp.bfloat16
     )
-    full_step = lax.all_gather(normalized, "grp", axis=1, tiled=True)
+    full_step = face_hold(normalized)
     update = jnp.dot(full_step, whole, preferred_element_type=jnp.float32)
     return (update, first_new, second_new)
 

time: 307 us -> 318 us (1.036)
  local copies, waits for them, and re-layouts: 0 us -> 10.1 us
    all_gather x0 -> x1, local copies, waits for them, and re-layouts: none -> 10.1 us  [form_screen(): return jnp.concatenate(lax.all_gather(w_in, across), axis=1)]
where the time goes in v1:
time: 318 us
  waiting for transfers between devices  239 us (75%)
  matrix products  46.3 us (15%)
  between operations  13.7 us (4%)
  local copies, waits for them, and re-layouts  10.1 us (3%)
  other arithmetic  7.72 us (2%)
    reduce_scatter x1, waiting for transfers between devices, body(): lax.psum_scatter(partial_value, 'grp', scatter_dimension=1, tiled=True)  109 us
    all_gather x1, waiting for transfers between devices, body(): whole = lax.all_gather(projector_t, 'fsdp', axis=0, tiled=True)  77.7 us
    all_gather x1, waiting for transfers between devices, form_screen(): return jnp.concatenate(lax.all_gather(w_in, across), axis=1)  52.5 us
    dot_general x1, matrix products, body(): update = jnp.dot(full_step, whole, preferred_element_type=jnp.float32)  24.5 us
    dot_general x1, matrix products, body(): lax.dot_general(grad, whole, (((1,), (1,)), ((), ())), preferred_element_...  21.8 us
    all_gather x1, local copies, waits for them, and re-layouts, form_screen(): return jnp.concatenate(lax.all_gather(w_in, across), axis=1)  10.1 us
    convert_element_type x1, other arithmetic, body(): (first_new / correct_one / (jnp.sqrt(second_new / correct_two) + 1e-08))....  7.72 us
  transfers between devices with their start and end apart: 3, of which 3 were waited for; matrix products, arithmetic and copies ran while one was open for 0% of the time, Pallas kernels for 0%

profile of v1, /device:TPU:0, one launch (start us, length us, event | category | flops | bytes accessed | tf_op | source)
XLA Modules:
  0.0 317.6 jit_solution(4256818274934709007)
XLA Ops:
  7.2 0.0 all-gather.4.cloned.1.call-start
  7.2 0.7 all-gather.4.cloned.1.call-update
  7.9 0.0 reduce-scatter.2.cloned.1.call-start
  7.9 77.7 %all-gather.4.cloned.1.call-done = bf16[1024,2048]{1,0:T(8,128)(2,1)} async-done(((bf16[128,2048]{1,0:T(8,128)(2,1)}), bf16[1024,2048]{1,0:T(8,128)(2,1)}) %all-gather.4.cloned.1.call-update) | async-done | bytes 4194320 | tf_op jit(solution)/shard_map/all_gather | solution.py:18
  85.6 21.8 %fusion.2 = f32[3584,1024]{1,0:T(8,128)} fusion(bf16[3584,2048]{1,0:T(8,128)(2,1)} %param.4, bf16[1024,2048]{1,0:T(8,128)(2,1)} %all-gather.4.cloned.1.call-done), kind=kOutput, calls=%fused_computation.4 | convolution fusion | flops 15032385536 | bytes 33554432 | tf_op jit(solution)/shard_map/dot_general | solution.py:19
  107.5 0.0 reduce-scatter.2.cloned.1.call-update
  107.5 0.2 all-gather.6.cloned.1.call-start
  107.7 108.5 %reduce-scatter.2.cloned.1.call-done = f32[3584,256]{1,0:T(8,128)} async-done(((f32[3584,1024]{1,0:T(8,128)}), f32[3584,256]{1,0:T(8,128)}) %reduce-scatter.2.cloned.1.call-update) | async-done | bytes 3670032 | tf_op jit(solution)/shard_map/reduce_scatter | solution.py:22
  216.3 7.7 %divide_convert_fusion = (bf16[3584,256]{1,0:T(8,128)(2,1)}, f32[3584,256]{1,0:T(8,128)}, f32[3584,256]{1,0:T(8,128)}) fusion(f32[3584,256]{1,0:T(8,128)} %reduce-scatter.2.cloned.1.call-done, f32[3584,256]{1,0:T(8,128)} %param.6, f32[3584,256]{1,0:T(8,128)} %param.7), kind=kLoop, calls=%fused_computation.2 | loop fusion | flops 11010048 | bytes 20185088 | tf_op jit(solution)/shard_map/convert_element_type | solution.py:27
  224.0 0.0 all-gather.6.cloned.1.call-update
  224.0 52.5 %all-gather.6.cloned.1.call-done = bf16[14336,256]{1,0:T(8,128)(2,1)} async-done(((bf16[3584,256]{1,0:T(8,128)(2,1)}), bf16[14336,256]{1,0:T(8,128)(2,1)}) %all-gather.6.cloned.1.call-update) | async-done | bytes 7340048 | tf_op jit(solution)/shard_map/all_gather | solution.py:11
  276.5 10.1 %copy.7 = bf16[4,3584,256]{1,2,0:T(8,128)(2,1)} copy(bf16[4,3584,256]{2,1,0:T(8,128)(2,1)} %bitcast.8) | data formatting | bytes 14680064 | tf_op jit(solution)/shard_map/all_gather | solution.py:11
  286.6 24.5 %fusion.3 = f32[3584,2048]{1,0:T(8,128)} fusion(bf16[3584,1024]{0,1:T(8,128)(2,1)} %bitcast.9, bf16[1024,2048]{1,0:T(8,128)(2,1)} %all-gather.4.cloned.1.call-done), kind=kOutput, calls=%fused_computation.5 | convolution fusion | flops 15032385536 | bytes 40894464 | tf_op jit(solution)/shard_map/dot_general | solution.py:31
Async XLA Ops:
  7.2 78.5 %all-gather.4.cloned.1.call-start = ((), (), s32[]{:S(2)}) async-start(), calls=%async_computation.1 | async-start | bytes 4718592 | tf_op jit(solution)/shard_map/all_gather | solution.py:18
  7.9 208.4 %reduce-scatter.2.cloned.1.call-start = ((), (), s32[]{:S(2)}) async-start(), calls=%async_computation.2 | async-start | bytes 18350080 | tf_op jit(solution)/shard_map/reduce_scatter | solution.py:22
  107.5 169.0 %all-gather.6.cloned.1.call-start = ((), (), s32[]{:S(2)}) async-start(), calls=%async_computation.3 | async-start | bytes 9175040 | tf_op jit(solution)/shard_map/all_gather | solution.py:11
Sparse Core Ops, SparseCore 0:
  10.1 75.4 all-gather.3
  107.6 108.5 reduce-scatter.1
  224.1 52.3 all-gather.5
